TPU v7x, 32 devices: a whole 2x2x4 slice. The times are simulated.
32 devices in a mesh: left: 8 (over y, x, core), right: 4 (over z).
Axes of the slice: x: 2, y: 2, z: 4, core: 2. Of those that a mesh axis runs over, the one named last changes fastest.
Arguments:
- signal: float32 [256, 256, 1024], P(None, 'left', 'right'), may hold values from -6 to 6
- symbol_x: float32 [256], replicated, may hold values from 0.3 to 3
- symbol_y: float32 [256], replicated, may hold values from 0.3 to 3
- symbol_z: float32 [1024], replicated, may hold values from 0.3 to 3
Outputs:
- spectrum: float32 [128, 128, 512], P('left', 'right')
All inputs are finite; a program needn't handle non-finite values.
Results may differ from a plain program's by a relative error of at most 0.000096.
Values sent between devices are 32-bit elements; how exact they have to be, the bound alone decides.
A program may use at most 128 MiB of HBM per device.

v0:
```python
import functools

import jax
import jax.numpy as jnp
import numpy as np
from jax import lax
from jax.experimental import pallas as pl
from jax.experimental.pallas import tpu as pltpu
from jax.sharding import PartitionSpec as P

MESH = pl.DeviceIdType.MESH
LANES = 128
ROWS = 8
LAG = 2
AHEAD = 2


def kept_table(count):
    rank = np.arange(count)
    odd = 2 * rank + 1
    angle = np.pi / (4 * count) * ((odd[:, None] * odd[None, : count // 2]) % (8 * count))
    return np.cos(angle) * (2.0 / count) ** 0.5


def two_halves(table):
    high = table.astype(np.float32).astype(jnp.bfloat16)
    rest = table - high.astype(np.float64)
    return np.stack([high, rest.astype(np.float32).astype(jnp.bfloat16)])


def split(values):
    high = values.astype(jnp.bfloat16)
    return high, (values - high.astype(jnp.float32)).astype(jnp.bfloat16)


def product(first, second):
    dot = functools.partial(jnp.dot, preferred_element_type=jnp.float32)
    return dot(first[0], second[0]) + (dot(first[0], second[1]) + dot(first[1], second[0]))


def kernel(
    lefts, rights, chunks,
    signal, table_x, table_y, table_z, symbol_x, symbol_y, symbol_z, out,
    held, tx, ty, tz, first, lines, second, pencils,
    held_sem, table_sem, send0, recv0, send1, recv1, send2, recv2,
):
    left, right = lax.axis_index("left"), lax.axis_index("right")
    tiles, blocks, size_x = held.shape[0], held.shape[1], held.shape[2]
    modes_x, own_y = first.shape[0], first.shape[2]
    share_x, size_y = lines.shape[1], lefts * own_y
    share_y = size_y // 2 // rights
    step = share_x // chunks
    width = blocks * LANES

    def tile_copy(t, b):
        return pltpu.make_async_copy(
            signal.at[:, pl.ds(t * ROWS, ROWS), pl.ds(b * LANES, LANES)],
            held.at[t, b], held_sem.at[t, b])

    copy_x = pltpu.make_async_copy(table_x, tx, table_sem.at[0])
    copy_y = pltpu.make_async_copy(table_y, ty, table_sem.at[1])
    copy_z = pltpu.make_async_copy(table_z, tz, table_sem.at[2])
    copy_x.start()
    for t in range(min(AHEAD, tiles)):
        for b in range(blocks):
            tile_copy(t, b).start()

    barrier = pltpu.get_barrier_semaphore()
    for o in range(1, lefts):
        pl.semaphore_signal(barrier, 1, device_id=(lax.rem(left + o, lefts), right), device_id_type=MESH)
    for o in range(1, rights):
        pl.semaphore_signal(barrier, 1, device_id=(left, lax.rem(right + o, rights)), device_id_type=MESH)

    copy_x.wait()

    def send_tile(t, o):
        to = lax.rem(left + o, lefts)
        return pltpu.make_async_remote_copy(
            src_ref=first.at[pl.ds(to * share_x, step), :, pl.ds(pl.multiple_of(t * ROWS, ROWS), ROWS), :],
            dst_ref=lines.at[left, pl.ds(0, step), :, pl.ds(pl.multiple_of(t * ROWS, ROWS), ROWS), :],
            send_sem=send0.at[o, t], recv_sem=recv0.at[o, t],
            device_id=(to, right), device_id_type=MESH)

    def send_left(c, o):
        to = lax.rem(left + o, lefts)
        return pltpu.make_async_remote_copy(
            src_ref=first.at[pl.ds(to * share_x + c * step, step)],
            dst_ref=lines.at[left, pl.ds(c * step, step)],
            send_sem=send1.at[o, c], recv_sem=recv1.at[o, c],
            device_id=(to, right), device_id_type=MESH)

    def send_right(c, o):
        to = lax.rem(right + o, rights)
        return pltpu.make_async_remote_copy(
            src_ref=second.at[pl.ds(c * step, step), pl.ds(pl.multiple_of(to * share_y, share_y), share_y), :],
            dst_ref=pencils.at[right, pl.ds(c * step, step)],
            send_sem=send2.at[o, c], recv_sem=recv2.at[o, c],
            device_id=(left, to), device_id_type=MESH)

    def stage1(t, carry):
        for b in range(blocks):
            tile_copy(t, b).wait()

        @pl.when(t + AHEAD < tiles)
        def _():
            for b in range(blocks):
                tile_copy(t + AHEAD, b).start()

        for y in range(ROWS):
            values = jnp.concatenate(
                [held.at[t, b].reshape(size_x * ROWS, LANES)[pl.ds(y, size_x, stride=ROWS), :] for b in range(blocks)],
                axis=1)
            result = product((tx[0], tx[1]), split(values))
            for b in range(blocks):
                first.reshape(modes_x * blocks * own_y, LANES)[
                    pl.ds(b * own_y + t * ROWS + y, modes_x, stride=blocks * own_y), :] = (
                    result[:, b * LANES : (b + 1) * LANES])

        @pl.when(t == 0)
        def _():
            pl.semaphore_wait(barrier, lefts + rights - 2)

        for o in range(1, lefts):
            send_tile(t, o).start()
        return carry

    def start1(c, carry):
        for o in range(1, lefts):
            send_left(c, o).start()
        return carry

    lax.fori_loop(0, tiles, stage1, 0)
    lax.fori_loop(1, chunks, start1, 0)
    copy_y.start()
    copy_z.start()

    def own1(x, carry):
        lines[left, x] = first[left * share_x + x]
        return carry

    lax.fori_loop(0, share_x, own1, 0)
    copy_y.wait()
    copy_z.wait()

    pick = lax.broadcasted_iota(jnp.int32, (share_y, symbol_y.shape[1]), 1) == (
        right * share_y + lax.broadcasted_iota(jnp.int32, (share_y, symbol_y.shape[1]), 0))
    part_y = jnp.sum(jnp.where(pick, symbol_y[...], 0.0), axis=1, keepdims=True)
    modes_z = out.shape[2]

    def stage23(c, carry):
        @pl.when(c < chunks)
        def _():
            @pl.when(c == 0)
            def _():
                for t in range(tiles):
                    for o in range(1, lefts):
                        send_tile(t, o).wait_recv()

            @pl.when(c > 0)
            def _():
                for o in range(1, lefts):
                    send_left(c, o).wait_recv()

            for s in range(step):
                x = c * step + s
                values = jnp.concatenate([lines[:, x, b].reshape(size_y, LANES) for b in range(blocks)], axis=1)
                result = product((ty[0], ty[1]), split(values))
                second[x] = result
            for o in range(1, rights):
                send_right(c, o).start()
            for s in range(step):
                x = c * step + s
                pencils[right, x] = second[x, pl.ds(pl.multiple_of(right * share_y, share_y), share_y), :]

        @pl.when(c >= LAG)
        def _():
            d = c - LAG
            for o in range(1, rights):
                send_right(d, o).wait_recv()
            values = jnp.concatenate(
                [pencils[p, pl.ds(d * step, step)].reshape(step * share_y, width) for p in range(rights)], axis=1)
            result = product(split(values), (tz[0], tz[1]))
            for s in range(step):
                x = d * step + s
                symbol = (symbol_x[left * share_x + x] + part_y) + symbol_z[:, :modes_z]
                out[x] = result[s * share_y : (s + 1) * share_y] * ((1.0 - 0.2 * symbol) / (1.0 + 0.2 * symbol))
        return carry

    lax.fori_loop(0, chunks + LAG, stage23, 0)

    def finish(c, carry):
        @pl.when(c > 0)
        def _():
            for o in range(1, lefts):
                send_left(c, o).wait_send()

        for o in range(1, rights):
            send_right(c, o).wait_send()
        return carry

    for t in range(tiles):
        for o in range(1, lefts):
            send_tile(t, o).wait_send()

    lax.fori_loop(0, chunks, finish, 0)


def body(lefts, rights, signal, symbol_x, symbol_y, symbol_z):
    size_x, own_y, own_z = signal.shape
    size_y, size_z = own_y * lefts, own_z * rights
    modes_x, modes_y, modes_z = size_x // 2, size_y // 2, size_z // 2
    share_x, share_y = modes_x // lefts, modes_y // rights
    chunks = min(8, share_x)
    blocks, tiles = own_z // LANES, own_y // ROWS
    table_x = two_halves(kept_table(size_x).T)
    table_y = two_halves(kept_table(size_y).T)
    table_z = two_halves(kept_table(size_z))
    vmem = pl.BlockSpec(memory_space=pltpu.VMEM)
    any_ = pl.BlockSpec(memory_space=pl.ANY)
    smem = pl.BlockSpec(memory_space=pltpu.SMEM)
    dma = pltpu.SemaphoreType.DMA
    return pl.pallas_call(
        functools.partial(kernel, lefts, rights, chunks),
        out_shape=jax.ShapeDtypeStruct((share_x, share_y, modes_z), jnp.float32),
        in_specs=[any_] * 4 + [smem, vmem, vmem],
        out_specs=vmem,
        scratch_shapes=[
            pltpu.VMEM((tiles, blocks, size_x, ROWS, LANES), jnp.float32),
            pltpu.VMEM(table_x.shape, jnp.bfloat16),
            pltpu.VMEM(table_y.shape, jnp.bfloat16),
            pltpu.VMEM(table_z.shape, jnp.bfloat16),
            pltpu.VMEM((modes_x, blocks, own_y, LANES), jnp.float32),
            pltpu.VMEM((lefts, share_x, blocks, own_y, LANES), jnp.float32),
            pltpu.VMEM((share_x, modes_y, own_z), jnp.float32),
            pltpu.VMEM((rights, share_x, share_y, own_z), jnp.float32),
            dma((tiles, blocks)),
            dma((3,)),
            dma((lefts, tiles)),
            dma((lefts, tiles)),
            dma((lefts, chunks)),
            dma((lefts, chunks)),
            dma((rights, chunks)),
            dma((rights, chunks)),
        ],
        compiler_params=pltpu.CompilerParams(
            collective_id=0, has_side_effects=True, vmem_limit_bytes=62 * 2**20),
    )(signal, table_x, table_y, table_z, symbol_x, symbol_y[None, :], symbol_z[None, :])


def solution(mesh):
    lefts, rights = mesh.shape["left"], mesh.shape["right"]
    in_specs = (P(None, "left", "right"), P(), P(), P())
    out_specs = P("left", "right", None)
    return jax.shard_map(
        functools.partial(body, lefts, rights), mesh=mesh, in_specs=in_specs, out_specs=out_specs, check_vma=False)
```

profile of v0, /device:TPU:0, one launch (start us, length us, event | category | flops | bytes accessed | tf_op | source)
XLA Modules:
  0.0 68.7 jit_solution(15798120360994047970)
XLA Ops:
  0.0 66.4 %shard_map.73 = f32[16,32,512]{2,1,0:T(8,128)} custom-call(f32[256,32,256]{2,1,0:T(8,128)} %signal.1, bf16[2,128,256]{2,1,0:T(8,128)(2,1)} %constant.4.clone.table_x.table_y, bf16[2,128,256]{2,1,0:T(8,128)(2,1)} %constant.4.clone.table_x.table_y, bf16[2,1024,512]{2,1,0:T(8,128)(2,1)} %constant.5.clone.table_z, f32[256]{0:T(256)} %symbol_x.1, ...), custom_call_target="tpu_custom_call" | custom-call | tf_op jit(solution)/shard_map/pallas_call | solution.py:222
  66.4 2.3 %copy.9 = f32[16,32,512]{2,1,0:T(8,128)} copy(f32[16,32,512]{2,1,0:T(8,128)} %shard_map.73) | data formatting | bytes 2097152
where the time goes:
time: 69 us; the launch traced here: 68.7 us
  Pallas kernels  66.4 us (96%)
  local copies, waits for them, and re-layouts  2.29 us (3%)
    pallas_call x1, Pallas kernels, body(): pl.pallas_call(functools.partial(kernel, lefts, rights, chunks), out_shap...  66.4 us
    unnamed x1, local copies, waits for them, and re-layouts  2.29 us

commit v1 on v0

v1 whole, which is shorter than its diff:
```python
import functools

import jax
import jax.numpy as jnp
import numpy as np
from jax import lax
from jax.experimental import pallas as pl
from jax.experimental.pallas import tpu as pltpu
from jax.sharding import PartitionSpec as P

MESH = pl.DeviceIdType.MESH
LANES = 128
ROWS = 8
AHEAD = 2
REST = 32


def kept_table(count):
    rank = np.arange(count)
    odd = 2 * rank + 1
    angle = np.pi / (4 * count) * ((odd[:, None] * odd[None, : count // 2]) % (8 * count))
    return np.cos(angle) * (2.0 / count) ** 0.5


def half_band_basis(count, keep):
    at = np.arange(1, count)
    off = at * (count - at) / 2.0
    columns = np.linalg.eigh(np.diag(off, 1) + np.diag(off, -1))[1][:, ::-1][:, :keep]
    peak = columns[np.abs(columns).argmax(axis=0), np.arange(keep)]
    return columns * np.where(peak < 0, -1.0, 1.0)


def two_halves(table):
    high = table.astype(np.float32).astype(jnp.bfloat16)
    rest = table - high.astype(np.float64)
    return np.stack([high, rest.astype(np.float32).astype(jnp.bfloat16)])


def split(values):
    high = values.astype(jnp.bfloat16)
    return high, (values - high.astype(jnp.float32)).astype(jnp.bfloat16)


def product(first, second):
    dot = functools.partial(jnp.dot, preferred_element_type=jnp.float32)
    return dot(first[0], second[0]) + (dot(first[0], second[1]) + dot(first[1], second[0]))


def kernel(
    lefts, rights, group, cuts,
    signal, table_x, table_y, table_v, table_w, symbol_x, symbol_y, symbol_z, out,
    held, tx, ty, tv, tw, spread, first, lines, second, pencils, done,
    held_sem, table_sem, send0, recv0, send1, recv1, send2, recv2, out_sem,
):
    left, right = lax.axis_index("left"), lax.axis_index("right")
    tiles, blocks, size_x = held.shape[0], held.shape[1], held.shape[2]
    modes_x = size_x // 2
    slots = lines.shape[2]
    share_x = done.shape[0]
    size_y = lefts * tiles * ROWS
    modes_y = size_y // 2
    share_y = modes_y // rights
    groups = share_x // group
    unit = group + 1
    rest = LANES // group
    begins = [sum(cuts[:k]) for k in range(len(cuts))]
    lane_group = lax.broadcasted_iota(jnp.int32, (ROWS, LANES), 1) // rest

    def tile_copy(t, b):
        return pltpu.make_async_copy(
            signal.at[:, pl.ds(t * ROWS, ROWS), pl.ds(b * LANES, LANES)],
            held.at[t, b], held_sem.at[t, b])

    copy_x = pltpu.make_async_copy(table_x, tx, table_sem.at[0])
    copy_v = pltpu.make_async_copy(table_v, tv, table_sem.at[1])
    copy_y = pltpu.make_async_copy(table_y, ty, table_sem.at[2])
    copy_w = pltpu.make_async_copy(table_w, tw, table_sem.at[3])
    copy_x.start()
    for t in range(min(AHEAD, tiles)):
        for b in range(blocks):
            tile_copy(t, b).start()
    copy_v.start()

    barrier = pltpu.get_barrier_semaphore()
    for o in range(1, lefts):
        pl.semaphore_signal(barrier, 1, device_id=(lax.bitwise_xor(left, o), right), device_id_type=MESH)
    for o in range(1, rights):
        pl.semaphore_signal(barrier, 1, device_id=(left, lax.bitwise_xor(right, o)), device_id_type=MESH)

    copy_x.wait()
    copy_v.wait()

    def send_tile(t, o):
        to = lax.bitwise_xor(left, o)
        return pltpu.make_async_remote_copy(
            src_ref=first.at[t, pl.ds(to * slots, cuts[0])],
            dst_ref=lines.at[left, t, pl.ds(0, cuts[0])],
            send_sem=send0.at[o, t], recv_sem=recv0.at[o, t],
            device_id=(to, right), device_id_type=MESH)

    def send_left(g, k, o):
        to = lax.bitwise_xor(left, o)
        at = g * unit + begins[k]
        return pltpu.make_async_remote_copy(
            src_ref=first.at[:, pl.ds(to * slots + at, cuts[k])],
            dst_ref=lines.at[left, :, pl.ds(at, cuts[k])],
            send_sem=send1.at[o, g, k], recv_sem=recv1.at[o, g, k],
            device_id=(to, right), device_id_type=MESH)

    def send_right(g, k, o):
        to = lax.bitwise_xor(right, o)
        at = g * unit + begins[k]
        return pltpu.make_async_remote_copy(
            src_ref=second.at[pl.ds(at, cuts[k]), pl.ds(pl.multiple_of(to * share_y, share_y), share_y), :],
            dst_ref=pencils.at[right, pl.ds(at, cuts[k])],
            send_sem=send2.at[o, g, k], recv_sem=recv2.at[o, g, k],
            device_id=(left, to), device_id_type=MESH)

    def result_copy(g):
        return pltpu.make_async_copy(
            done.at[pl.ds(g * group, group)], out.at[pl.ds(g * group, group)], out_sem.at[g])

    def stage1(t, carry):
        for b in range(blocks):
            tile_copy(t, b).wait()

        @pl.when(t + AHEAD < tiles)
        def _():
            for b in range(blocks):
                tile_copy(t + AHEAD, b).start()

        parts = []
        for y in range(ROWS):
            values = jnp.concatenate(
                [held.at[t, b].reshape(size_x * ROWS, LANES)[pl.ds(y, size_x, stride=ROWS), :] for b in range(blocks)],
                axis=1)
            parts.append(product((tx[0], tx[1]), split(values)))
        result = product(split(jnp.concatenate(parts, axis=0)), (tv[0], tv[1]))
        for y in range(ROWS):
            for b in range(2):
                spread.at[b].reshape(modes_x * ROWS, LANES)[pl.ds(y, modes_x, stride=ROWS), :] = (
                    result[y * modes_x : (y + 1) * modes_x, b * LANES : (b + 1) * LANES])

        def place(n, carry):
            packed = spread[1, n * group]
            for j in range(1, group):
                packed = jnp.where(lane_group == j, spread[1, n * group + j], packed)
            first[t, n * unit] = packed
            for j in range(group):
                first[t, n * unit + 1 + j] = spread[0, n * group + j]
            return carry

        lax.fori_loop(0, modes_x // group, place, 0, unroll=4)

        @pl.when(t == 0)
        def _():
            pl.semaphore_wait(barrier, lefts + rights - 2)

        for o in range(lefts - 1, 0, -1):
            send_tile(t, o).start()
        return carry

    lax.fori_loop(0, tiles, stage1, 0)

    def start1(g, carry):
        for k in range(len(cuts)):
            def start():
                for o in range(lefts - 1, 0, -1):
                    send_left(g, k, o).start()

            if k == 0:
                pl.when(g > 0)(start)
            else:
                start()
        return carry

    lax.fori_loop(0, groups, start1, 0)
    copy_y.start()
    copy_w.start()

    def own1(s, carry):
        for t in range(tiles):
            lines[left, t, s] = first[t, left * slots + s]
        return carry

    lax.fori_loop(0, slots, own1, 0)
    copy_y.wait()
    copy_w.wait()

    pick = lax.broadcasted_iota(jnp.int32, (share_y, symbol_y.shape[1]), 1) == (
        right * share_y + lax.broadcasted_iota(jnp.int32, (share_y, symbol_y.shape[1]), 0))
    part_y = jnp.sum(jnp.where(pick, symbol_y[...], 0.0), axis=1, keepdims=True)
    modes_z = done.shape[2]
    wide_group = lax.broadcasted_iota(jnp.int32, (share_y, LANES), 1) // rest

    def stage23(g, carry):
        @pl.when(g < groups)
        def _():
            for k in range(len(cuts)):
                def wait_left():
                    for o in range(lefts - 1, 0, -1):
                        send_left(g, k, o).wait_recv()

                if k == 0:
                    pl.when(g > 0)(wait_left)

                    @pl.when(g == 0)
                    def _():
                        for t in range(tiles):
                            for o in range(1, lefts):
                                send_tile(t, o).wait_recv()
                else:
                    wait_left()

                at = g * unit + begins[k]
                values = jnp.concatenate(
                    [lines[:, :, at + s].reshape(size_y, LANES) for s in range(cuts[k])], axis=1)
                result = product((ty[0], ty[1]), split(values))
                for s in range(cuts[k]):
                    second[at + s] = result[:, s * LANES : (s + 1) * LANES]
                for o in range(rights - 1, 0, -1):
                    send_right(g, k, o).start()
                for s in range(cuts[k]):
                    pencils[right, at + s] = second[at + s, pl.ds(pl.multiple_of(right * share_y, share_y), share_y), :]

        @pl.when(g >= 1)
        def _():
            d = g - 1
            for k in range(len(cuts)):
                for o in range(1, rights):
                    send_right(d, k, o).wait_recv()
            columns = []
            for p in range(rights):
                columns.append(pencils[p, pl.ds(d * unit + 1, group)].reshape(group * share_y, LANES))
                packed = pencils[p, d * unit]
                columns.append(jnp.concatenate([jnp.where(wide_group == j, packed, 0.0) for j in range(group)], axis=0))
            result = product(split(jnp.concatenate(columns, axis=1)), (tw[0], tw[1]))
            for s in range(group):
                x = d * group + s
                symbol = (symbol_x[left * share_x + x] + part_y) + symbol_z[:, :modes_z]
                done[x] = result[s * share_y : (s + 1) * share_y] * ((1.0 - 0.2 * symbol) / (1.0 + 0.2 * symbol))
            result_copy(d).start()
        return carry

    lax.fori_loop(0, groups + 1, stage23, 0)

    for t in range(tiles):
        for o in range(1, lefts):
            send_tile(t, o).wait_send()

    def finish(g, carry):
        for k in range(len(cuts)):
            def wait_left():
                for o in range(1, lefts):
                    send_left(g, k, o).wait_send()

            if k == 0:
                pl.when(g > 0)(wait_left)
            else:
                wait_left()
            for o in range(1, rights):
                send_right(g, k, o).wait_send()
        result_copy(g).wait()
        return carry

    lax.fori_loop(0, groups, finish, 0)


def body(lefts, rights, signal, symbol_x, symbol_y, symbol_z):
    size_x, own_y, own_z = signal.shape
    size_y, size_z = own_y * lefts, own_z * rights
    modes_x, modes_y, modes_z = size_x // 2, size_y // 2, size_z // 2
    share_x, share_y = modes_x // lefts, modes_y // rights
    blocks, tiles = own_z // LANES, own_y // ROWS
    group = LANES // REST
    groups = share_x // group
    slots = share_x + groups
    cuts = (2, group - 1)
    basis = half_band_basis(own_z, LANES + REST)
    table_x = two_halves(kept_table(size_x).T)
    table_y = two_halves(kept_table(size_y).T)
    table_v = two_halves(np.concatenate([basis[:, :LANES]] + [basis[:, LANES:]] * group, axis=1))
    rows = np.einsum("ic,pik->pck", basis, kept_table(size_z).reshape(rights, own_z, modes_z))
    table_w = two_halves(
        np.concatenate([rows[:, :LANES]] + [rows[:, LANES:]] * group, axis=1).reshape(rights * 2 * LANES, modes_z))
    vmem = pl.BlockSpec(memory_space=pltpu.VMEM)
    any_ = pl.BlockSpec(memory_space=pl.ANY)
    smem = pl.BlockSpec(memory_space=pltpu.SMEM)
    dma = pltpu.SemaphoreType.DMA
    return pl.pallas_call(
        functools.partial(kernel, lefts, rights, group, cuts),
        out_shape=jax.ShapeDtypeStruct((share_x, share_y, modes_z), jnp.float32),
        in_specs=[any_] * 5 + [smem, vmem, vmem],
        out_specs=any_,
        scratch_shapes=[
            pltpu.VMEM((tiles, blocks, size_x, ROWS, LANES), jnp.float32),
            pltpu.VMEM(table_x.shape, jnp.bfloat16),
            pltpu.VMEM(table_y.shape, jnp.bfloat16),
            pltpu.VMEM(table_v.shape, jnp.bfloat16),
            pltpu.VMEM(table_w.shape, jnp.bfloat16),
            pltpu.VMEM((2, modes_x, ROWS, LANES), jnp.float32),
            pltpu.VMEM((tiles, lefts * slots, ROWS, LANES), jnp.float32),
            pltpu.VMEM((lefts, tiles, slots, ROWS, LANES), jnp.float32),
            pltpu.VMEM((slots, modes_y, LANES), jnp.float32),
            pltpu.VMEM((rights, slots, share_y, LANES), jnp.float32),
            pltpu.VMEM((share_x, share_y, modes_z), jnp.float32),
            dma((tiles, blocks)),
            dma((4,)),
            dma((lefts, tiles)),
            dma((lefts, tiles)),
            dma((lefts, groups, len(cuts))),
            dma((lefts, groups, len(cuts))),
            dma((rights, groups, len(cuts))),
            dma((rights, groups, len(cuts))),
            dma((groups,)),
        ],
        compiler_params=pltpu.CompilerParams(
            collective_id=0, has_side_effects=True, vmem_limit_bytes=62 * 2**20),
    )(signal, table_x, table_y, table_v, table_w, symbol_x, symbol_y[None, :], symbol_z[None, :])


def solution(mesh):
    lefts, rights = mesh.shape["left"], mesh.shape["right"]
    in_specs = (P(None, "left", "right"), P(), P(), P())
    out_specs = P("left", "right", None)
    return jax.shard_map(
        functools.partial(body, lefts, rights), mesh=mesh, in_specs=in_specs, out_specs=out_specs, check_vma=False)
```

time: 69 us -> 53 us (0.77)
  Pallas kernels: 66.4 us -> 50.5 us
    pallas_call x1, Pallas kernels: 66.4 us -> 50.5 us  [body(): pl.pallas_call(functools.partial(kernel, lefts, rights, group, cuts), out...]
where the time goes in v1:
time: 53 us; the launch traced here: 52.8 us
  Pallas kernels  50.5 us (95%)
  local copies, waits for them, and re-layouts  2.29 us (4%)
    pallas_call x1, Pallas kernels, body(): pl.pallas_call(functools.partial(kernel, lefts, rights, group, cuts), out...  50.5 us
    unnamed x1, local copies, waits for them, and re-layouts  2.29 us

profile of v1, /device:TPU:0, one launch (start us, length us, event | category | flops | bytes accessed | tf_op | source)
XLA Modules:
  0.0 52.8 jit_solution(8491626492066300671)
XLA Ops:
  0.0 50.5 %shard_map.82 = f32[16,32,512]{2,1,0:T(8,128)} custom-call(f32[256,32,256]{2,1,0:T(8,128)} %signal.1, bf16[2,128,256]{2,1,0:T(8,128)(2,1)} %constant.6.clone.table_x.table_y, bf16[2,128,256]{2,1,0:T(8,128)(2,1)} %constant.6.clone.table_x.table_y, bf16[2,256,256]{2,1,0:T(8,128)(2,1)} %constant.7.clone.table_v, bf16[2,1024,512]{2,1,0:T(8,128)(2,1)} %constant.8.clone.table_w, ...), custom_call_target="tpu_custom_call" | custom-call | tf_op jit(solution)/shard_map/pallas_call | solution.py:290
  50.5 2.3 %copy.10 = f32[16,32,512]{2,1,0:T(8,128)} copy(f32[16,32,512]{2,1,0:T(8,128)} %shard_map.82) | data formatting | bytes 2097152

commit v2 on v1

v2 whole, which is shorter than its diff:
```python
import functools

import jax
import jax.numpy as jnp
import numpy as np
from jax import lax
from jax.experimental import pallas as pl
from jax.experimental.pallas import tpu as pltpu
from jax.sharding import PartitionSpec as P

MESH = pl.DeviceIdType.MESH
LANES = 128
ROWS = 8
AHEAD = 2
EARLY = 2
REST = 32


def kept_table(count):
    rank = np.arange(count)
    odd = 2 * rank + 1
    angle = np.pi / (4 * count) * ((odd[:, None] * odd[None, : count // 2]) % (8 * count))
    return np.cos(angle) * (2.0 / count) ** 0.5


def half_band_basis(count, keep):
    at = np.arange(1, count)
    off = at * (count - at) / 2.0
    columns = np.linalg.eigh(np.diag(off, 1) + np.diag(off, -1))[1][:, ::-1][:, :keep]
    peak = columns[np.abs(columns).argmax(axis=0), np.arange(keep)]
    return columns * np.where(peak < 0, -1.0, 1.0)


def two_halves(table):
    high = table.astype(np.float32).astype(jnp.bfloat16)
    rest = table - high.astype(np.float64)
    return np.stack([high, rest.astype(np.float32).astype(jnp.bfloat16)])


def split(values):
    high = values.astype(jnp.bfloat16)
    return high, (values - high.astype(jnp.float32)).astype(jnp.bfloat16)


def product(first, second):
    dot = functools.partial(jnp.dot, preferred_element_type=jnp.float32)
    rows = first.shape[0] // 2
    both = dot(first, second[0])
    return both[:rows] + (dot(first[:rows], second[1]) + both[rows:])


def stacked(values):
    return jnp.concatenate(split(values), axis=0)


def kernel(
    lefts, rights, group, cuts,
    signal, table_x, table_y, table_v, table_w, symbol_x, symbol_y, symbol_z, out,
    held, halves, tx, ty, tv, tw, first, lines, second, pencils, done,
    held_sem, table_sem, sent_left, sent_right, came_left, came_right, out_sem,
):
    left, right = lax.axis_index("left"), lax.axis_index("right")
    tiles, blocks, size_x = held.shape[0], held.shape[1], held.shape[2]
    groups, unit = first.shape[1], first.shape[2]
    share_x = done.shape[0]
    size_y = lefts * tiles * ROWS
    modes_y = size_y // 2
    share_y = modes_y // rights
    rest = LANES // group
    rows_g = group * lefts
    early = min(EARLY, groups)
    begins = [sum(cuts[:k]) for k in range(len(cuts))]
    pieces = range(len(cuts))
    lane_group = lax.broadcasted_iota(jnp.int32, (lefts, LANES), 1) // rest

    def tile_copy(t, b):
        return pltpu.make_async_copy(
            signal.at[:, pl.ds(t * ROWS, ROWS), pl.ds(b * LANES, LANES)],
            held.at[t, b], held_sem.at[t, b])

    copy_x = pltpu.make_async_copy(table_x, tx, table_sem.at[0])
    copy_v = pltpu.make_async_copy(table_v, tv, table_sem.at[1])
    copy_y = pltpu.make_async_copy(table_y, ty, table_sem.at[2])
    copy_w = pltpu.make_async_copy(table_w, tw, table_sem.at[3])
    copy_x.start()
    for t in range(min(AHEAD, tiles)):
        for b in range(blocks):
            tile_copy(t, b).start()
    copy_v.start()

    barrier = pltpu.get_barrier_semaphore()
    for o in range(1, lefts):
        pl.semaphore_signal(barrier, 1, device_id=(lax.bitwise_xor(left, o), right), device_id_type=MESH)
    for o in range(1, rights):
        pl.semaphore_signal(barrier, 1, device_id=(left, lax.bitwise_xor(right, o)), device_id_type=MESH)

    copy_x.wait()
    copy_v.wait()

    def send_tile(t, g, k, o):
        to = lax.bitwise_xor(left, o)
        return pltpu.make_async_remote_copy(
            src_ref=first.at[t, g, pl.ds(begins[k], cuts[k]), to],
            dst_ref=lines.at[left, t, pl.ds(g * unit + begins[k], cuts[k])],
            send_sem=sent_left.at[0], recv_sem=came_left.at[g, k],
            device_id=(to, right), device_id_type=MESH)

    def send_left(g, k, o):
        to = lax.bitwise_xor(left, o)
        return pltpu.make_async_remote_copy(
            src_ref=first.at[:, g, pl.ds(begins[k], cuts[k]), to],
            dst_ref=lines.at[left, :, pl.ds(g * unit + begins[k], cuts[k])],
            send_sem=sent_left.at[0], recv_sem=came_left.at[g, k],
            device_id=(to, right), device_id_type=MESH)

    def send_right(g, k, o):
        to = lax.bitwise_xor(right, o)
        at = g * unit + begins[k]
        return pltpu.make_async_remote_copy(
            src_ref=second.at[pl.ds(at, cuts[k]), pl.ds(pl.multiple_of(to * share_y, share_y), share_y), :],
            dst_ref=pencils.at[right, pl.ds(at, cuts[k])],
            send_sem=sent_right.at[0], recv_sem=came_right.at[o, g],
            device_id=(left, to), device_id_type=MESH)

    def all_left(k_at, k_count, recv):
        part = lines.at[pl.ds(0, lefts - 1), :, pl.ds(k_at, k_count)]
        return pltpu.make_async_remote_copy(
            src_ref=part, dst_ref=part, send_sem=sent_left.at[0], recv_sem=recv,
            device_id=(lax.bitwise_xor(left, 1), right), device_id_type=MESH)

    def wait_left(g, k):
        all_left(g * unit + begins[k], cuts[k], came_left.at[g, k]).wait_recv()

    def wait_right(g, o):
        part = pencils.at[0, pl.ds(g * unit, unit)]
        pltpu.make_async_remote_copy(
            src_ref=part, dst_ref=part, send_sem=sent_right.at[0], recv_sem=came_right.at[o, g],
            device_id=(left, lax.bitwise_xor(right, o)), device_id_type=MESH).wait_recv()

    def result_copy(g):
        return pltpu.make_async_copy(
            done.at[pl.ds(g * group, group)], out.at[pl.ds(g * group, group)], out_sem.at[g])

    def transform(t, low, high, piece):
        parts = []
        for y in range(ROWS):
            parts.append(product(tx[pl.ds(2 * low * rows_g, 2 * (high - low) * rows_g), :], piece(y)))
        result = product(stacked(jnp.concatenate(parts, axis=0)), (tv[0], tv[1]))
        for y in range(ROWS):
            for g in range(low, high):
                view = first.at[t, g].reshape(unit * lefts * ROWS, LANES)
                packed = None
                for j in range(group):
                    at = ((y * (high - low) + g - low) * group + j) * lefts
                    rows = result[at : at + lefts]
                    view[pl.ds((1 + j) * lefts * ROWS + y, lefts, stride=ROWS), :] = rows[:, :LANES]
                    packed = rows[:, LANES:] if j == 0 else jnp.where(lane_group == j, rows[:, LANES:], packed)
                view[pl.ds(y, lefts, stride=ROWS), :] = packed

    def send_tiles(t, g):
        for k in pieces:
            for o in range(lefts - 1, 0, -1):
                send_tile(t, g, k, o).start()

    def stage1(t, carry):
        for b in range(blocks):
            tile_copy(t, b).wait()

        @pl.when(t + AHEAD < tiles)
        def _():
            for b in range(blocks):
                tile_copy(t + AHEAD, b).start()

        def piece(y):
            values = jnp.concatenate(
                [held.at[t, b].reshape(size_x * ROWS, LANES)[pl.ds(y, size_x, stride=ROWS), :] for b in range(blocks)],
                axis=1)
            both = split(values)
            halves[t, y, 0] = both[0]
            halves[t, y, 1] = both[1]
            return both

        transform(t, 0, 1, piece)

        @pl.when(t == 0)
        def _():
            pl.semaphore_wait(barrier, lefts + rights - 2)
            copy_y.start()
            copy_w.start()

        send_tiles(t, 0)
        return carry

    lax.fori_loop(0, tiles, stage1, 0)
    copy_y.wait()

    def own(g):
        for t in range(tiles):
            for s in range(unit):
                lines[left, t, g * unit + s] = first[t, g, s, left]

    def stage2(g, k):
        at = g * unit + begins[k]
        values = jnp.concatenate(
            [lines[:, :, at + s].reshape(size_y, LANES) for s in range(cuts[k])], axis=1)
        result = product(ty[...], split(values))
        for s in range(cuts[k]):
            second[at + s] = result[:, s * LANES : (s + 1) * LANES]
        for o in range(rights - 1, 0, -1):
            send_right(g, k, o).start()
        for s in range(cuts[k]):
            pencils[right, at + s] = second[at + s, pl.ds(pl.multiple_of(right * share_y, share_y), share_y), :]

    own(0)

    def later1(t, carry):
        transform(t, 1, groups, lambda y: (halves[t, y, 0], halves[t, y, 1]))
        for g in range(1, early):
            send_tiles(t, g)
        for k in pieces:
            @pl.when(t == min(1 + k, tiles - 1))
            def _():
                wait_left(0, k)
                stage2(0, k)
        return carry

    lax.fori_loop(0, tiles, later1, 0)

    def start1(g, carry):
        for k in pieces:
            for o in range(lefts - 1, 0, -1):
                send_left(g, k, o).start()
        return carry

    lax.fori_loop(early, groups, start1, 0)
    copy_w.wait()

    pick = lax.broadcasted_iota(jnp.int32, (share_y, symbol_y.shape[1]), 1) == (
        right * share_y + lax.broadcasted_iota(jnp.int32, (share_y, symbol_y.shape[1]), 0))
    part_y = jnp.sum(jnp.where(pick, symbol_y[...], 0.0), axis=1, keepdims=True)
    modes_z = done.shape[2]
    wide_group = lax.broadcasted_iota(jnp.int32, (share_y, LANES), 1) // rest

    def stage3(g):
        for s in range(group):
            x = g * group + s
            symbol = (symbol_x[left * share_x + x] + part_y) + symbol_z[:, :modes_z]
            done[x] = (1.0 - 0.2 * symbol) / (1.0 + 0.2 * symbol)
        total = None
        for o in range(rights):
            if o > 0:
                wait_right(g, o)
            p = lax.bitwise_xor(right, o)
            main = pencils[p, pl.ds(g * unit + 1, group)].reshape(group * share_y, LANES)
            packed = pencils[p, g * unit]
            other = jnp.concatenate([jnp.where(wide_group == j, packed, 0.0) for j in range(group)], axis=0)
            at = pl.ds(pl.multiple_of(p * 2 * LANES, 2 * LANES), 2 * LANES)
            part = product(stacked(jnp.concatenate([main, other], axis=1)), (tw[0, at, :], tw[1, at, :]))
            total = part if total is None else total + part
        for s in range(group):
            x = g * group + s
            done[x] = total[s * share_y : (s + 1) * share_y] * done[x]
        result_copy(g).start()

    def stage23(g, carry):
        @pl.when(g < groups)
        def _():
            own(g)
            for k in pieces:
                wait_left(g, k)
                stage2(g, k)

        stage3(g - 1)
        return carry

    lax.fori_loop(1, groups + 1, stage23, 0)

    all_left(0, groups * unit, came_left.at[0, 0]).wait_send()
    part = pencils.at[pl.ds(0, rights - 1)]
    pltpu.make_async_remote_copy(
        src_ref=part, dst_ref=part, send_sem=sent_right.at[0], recv_sem=came_right.at[0, 0],
        device_id=(left, lax.bitwise_xor(right, 1)), device_id_type=MESH).wait_send()

    def finish(g, carry):
        result_copy(g).wait()
        return carry

    lax.fori_loop(0, groups, finish, 0)


def body(lefts, rights, signal, symbol_x, symbol_y, symbol_z):
    size_x, own_y, own_z = signal.shape
    size_y, size_z = own_y * lefts, own_z * rights
    modes_x, modes_y, modes_z = size_x // 2, size_y // 2, size_z // 2
    share_x, share_y = modes_x // lefts, modes_y // rights
    blocks, tiles = own_z // LANES, own_y // ROWS
    group = LANES // REST
    groups = share_x // group
    slots = share_x + groups
    cuts = (2, group - 1)
    basis = half_band_basis(own_z, LANES + REST)
    rows_x = kept_table(size_x).T.reshape(lefts, groups, group, size_x).transpose(1, 2, 0, 3)
    rows_x = rows_x.reshape(groups, group * lefts, size_x)
    table_x = np.concatenate(
        [np.concatenate(two_halves(np.concatenate(part))) for part in (rows_x[:1], rows_x[1:])])
    table_y = np.concatenate(two_halves(kept_table(size_y).T))
    table_v = two_halves(np.concatenate([basis[:, :LANES]] + [basis[:, LANES:]] * group, axis=1))
    rows = np.einsum("ic,pik->pck", basis, kept_table(size_z).reshape(rights, own_z, modes_z))
    table_w = two_halves(
        np.concatenate([rows[:, :LANES]] + [rows[:, LANES:]] * group, axis=1).reshape(rights * 2 * LANES, modes_z))
    vmem = pl.BlockSpec(memory_space=pltpu.VMEM)
    hbm = pl.BlockSpec(memory_space=pltpu.HBM)
    smem = pl.BlockSpec(memory_space=pltpu.SMEM)
    dma = pltpu.SemaphoreType.DMA
    return pl.pallas_call(
        functools.partial(kernel, lefts, rights, group, cuts),
        out_shape=jax.ShapeDtypeStruct((share_x, share_y, modes_z), jnp.float32),
        in_specs=[hbm] * 5 + [smem, vmem, vmem],
        out_specs=hbm,
        scratch_shapes=[
            pltpu.VMEM((tiles, blocks, size_x, ROWS, LANES), jnp.float32),
            pltpu.VMEM((tiles, ROWS, 2, size_x, own_z), jnp.bfloat16),
            pltpu.VMEM(table_x.shape, jnp.bfloat16),
            pltpu.VMEM(table_y.shape, jnp.bfloat16),
            pltpu.VMEM(table_v.shape, jnp.bfloat16),
            pltpu.VMEM(table_w.shape, jnp.bfloat16),
            pltpu.VMEM((tiles, groups, group + 1, lefts, ROWS, LANES), jnp.float32),
            pltpu.VMEM((lefts, tiles, slots, ROWS, LANES), jnp.float32),
            pltpu.VMEM((slots, modes_y, LANES), jnp.float32),
            pltpu.VMEM((rights, slots, share_y, LANES), jnp.float32),
            pltpu.VMEM((share_x, share_y, modes_z), jnp.float32),
            dma((tiles, blocks)),
            dma((4,)),
            dma((1,)),
            dma((1,)),
            dma((groups, len(cuts))),
            dma((rights, groups)),
            dma((groups,)),
        ],
        compiler_params=pltpu.CompilerParams(
            collective_id=0, has_side_effects=True, vmem_limit_bytes=62 * 2**20),
    )(signal, table_x, table_y, table_v, table_w, symbol_x, symbol_y[None, :], symbol_z[None, :])


def solution(mesh):
    lefts, rights = mesh.shape["left"], mesh.shape["right"]
    in_specs = (P(None, "left", "right"), P(), P(), P())
    out_specs = P("left", "right", None)
    return jax.shard_map(
        functools.partial(body, lefts, rights), mesh=mesh, in_specs=in_specs, out_specs=out_specs, check_vma=False)
```

time: 53 us -> 50.6 us (0.955)
  Pallas kernels: 50.5 us -> 48.1 us
    pallas_call x1, Pallas kernels: 50.5 us -> 48.1 us  [body(): pl.pallas_call(functools.partial(kernel, lefts, rights, group, cuts), out...]
where the time goes in v2:
time: 50.6 us; the launch traced here: 50.4 us
  Pallas kernels  48.1 us (95%)
  local copies, waits for them, and re-layouts  2.29 us (5%)
    pallas_call x1, Pallas kernels, body(): pl.pallas_call(functools.partial(kernel, lefts, rights, group, cuts), out...  48.1 us
    unnamed x1, local copies, waits for them, and re-layouts  2.29 us

profile of v2, /device:TPU:0, one launch (start us, length us, event | category | flops | bytes accessed | tf_op | source)
XLA Modules:
  0.0 50.4 jit_solution(16128093208351216098)
XLA Ops:
  0.0 48.1 %shard_map.82 = f32[16,32,512]{2,1,0:T(8,128)} custom-call(f32[256,32,256]{2,1,0:T(8,128)} %signal.1, bf16[256,256]{1,0:T(8,128)(2,1)} %constant.8.clone.table_x, bf16[256,256]{1,0:T(8,128)(2,1)} %constant.9.clone.table_y, bf16[2,256,256]{2,1,0:T(8,128)(2,1)} %constant.10.clone.table_v, bf16[2,1024,512]{2,1,0:T(8,128)(2,1)} %constant.11.clone.table_w, ...), custom_call_target="tpu_custom_call" | custom-call | tf_op jit(solution)/shard_map/pallas_call | solution.py:315
  48.1 2.3 %copy.10 = f32[16,32,512]{2,1,0:T(8,128)} copy(f32[16,32,512]{2,1,0:T(8,128)} %shard_map.82) | data formatting | bytes 2097152

commit v3 on v2

--- a/solution.py
+++ b/solution.py
@@ -12,7 +12,6 @@
 LANES = 128
 ROWS = 8
 AHEAD = 2
-EARLY = 2
 REST = 32
 
 
@@ -68,7 +67,6 @@
     share_y = modes_y // rights
     rest = LANES // group
     rows_g = group * lefts
-    early = min(EARLY, groups)
     begins = [sum(cuts[:k]) for k in range(len(cuts))]
     pieces = range(len(cuts))
     lane_group = lax.broadcasted_iota(jnp.int32, (lefts, LANES), 1) // rest
@@ -83,9 +81,8 @@
     copy_y = pltpu.make_async_copy(table_y, ty, table_sem.at[2])
     copy_w = pltpu.make_async_copy(table_w, tw, table_sem.at[3])
     copy_x.start()
-    for t in range(min(AHEAD, tiles)):
-        for b in range(blocks):
-            tile_copy(t, b).start()
+    for b in range(blocks):
+        tile_copy(0, b).start()
     copy_v.start()
 
     barrier = pltpu.get_barrier_semaphore()
@@ -96,13 +93,16 @@
 
     copy_x.wait()
     copy_v.wait()
-
-    def send_tile(t, g, k, o):
+    for t in range(1, min(AHEAD, tiles)):
+        for b in range(blocks):
+            tile_copy(t, b).start()
+
+    def send_tile(t, o):
         to = lax.bitwise_xor(left, o)
         return pltpu.make_async_remote_copy(
-            src_ref=first.at[t, g, pl.ds(begins[k], cuts[k]), to],
-            dst_ref=lines.at[left, t, pl.ds(g * unit + begins[k], cuts[k])],
-            send_sem=sent_left.at[0], recv_sem=came_left.at[g, k],
+            src_ref=first.at[t, 0, pl.ds(0, cuts[0]), to],
+            dst_ref=lines.at[left, t, pl.ds(0, cuts[0])],
+            send_sem=sent_left.at[0], recv_sem=came_left.at[0, 0],
             device_id=(to, right), device_id_type=MESH)
 
     def send_left(g, k, o):
@@ -157,10 +157,9 @@
                     packed = rows[:, LANES:] if j == 0 else jnp.where(lane_group == j, rows[:, LANES:], packed)
                 view[pl.ds(y, lefts, stride=ROWS), :] = packed
 
-    def send_tiles(t, g):
-        for k in pieces:
-            for o in range(lefts - 1, 0, -1):
-                send_tile(t, g, k, o).start()
+    def send_group(g, k):
+        for o in range(lefts - 1, 0, -1):
+            send_left(g, k, o).start()
 
     def stage1(t, carry):
         for b in range(blocks):
@@ -188,10 +187,13 @@
             copy_y.start()
             copy_w.start()
 
-        send_tiles(t, 0)
+        for o in range(lefts - 1, 0, -1):
+            send_tile(t, o).start()
         return carry
 
     lax.fori_loop(0, tiles, stage1, 0)
+    for k in pieces[1:]:
+        send_group(0, k)
     copy_y.wait()
 
     def own(g):
@@ -215,24 +217,22 @@
 
     def later1(t, carry):
         transform(t, 1, groups, lambda y: (halves[t, y, 0], halves[t, y, 1]))
-        for g in range(1, early):
-            send_tiles(t, g)
-        for k in pieces:
-            @pl.when(t == min(1 + k, tiles - 1))
-            def _():
-                wait_left(0, k)
-                stage2(0, k)
+
+        @pl.when(t == min(1, tiles - 1))
+        def _():
+            wait_left(0, 0)
+            stage2(0, 0)
+
         return carry
 
     lax.fori_loop(0, tiles, later1, 0)
 
     def start1(g, carry):
         for k in pieces:
-            for o in range(lefts - 1, 0, -1):
-                send_left(g, k, o).start()
-        return carry
-
-    lax.fori_loop(early, groups, start1, 0)
+            send_group(g, k)
+        return carry
+
+    lax.fori_loop(1, groups, start1, 0)
     copy_w.wait()
 
     pick = lax.broadcasted_iota(jnp.int32, (share_y, symbol_y.shape[1]), 1) == (
@@ -265,15 +265,23 @@
     def stage23(g, carry):
         @pl.when(g < groups)
         def _():
-            own(g)
-            for k in pieces:
+            @pl.when(g > 0)
+            def _():
+                own(g)
+                wait_left(g, 0)
+                stage2(g, 0)
+
+            for k in pieces[1:]:
                 wait_left(g, k)
                 stage2(g, k)
 
-        stage3(g - 1)
-        return carry
-
-    lax.fori_loop(1, groups + 1, stage23, 0)
+        @pl.when(g > 0)
+        def _():
+            stage3(g - 1)
+
+        return carry
+
+    lax.fori_loop(0, groups + 1, stage23, 0)
 
     all_left(0, groups * unit, came_left.at[0, 0]).wait_send()
     part = pencils.at[pl.ds(0, rights - 1)]
@@ -297,7 +305,7 @@
     group = LANES // REST
     groups = share_x // group
     slots = share_x + groups
-    cuts = (2, group - 1)
+    cuts = (2, 2, 1)
     basis = half_band_basis(own_z, LANES + REST)
     rows_x = kept_table(size_x).T.reshape(lefts, groups, group, size_x).transpose(1, 2, 0, 3)
     rows_x = rows_x.reshape(groups, group * lefts, size_x)

time: 50.6 us -> 48.9 us (0.966)
  Pallas kernels: 48.1 us -> 46.4 us
    pallas_call x1, Pallas kernels: 48.1 us -> 46.4 us  [body(): pl.pallas_call(functools.partial(kernel, lefts, rights, group, cuts), out...]
where the time goes in v3:
time: 48.9 us; the launch traced here: 48.7 us
  Pallas kernels  46.4 us (95%)
  local copies, waits for them, and re-layouts  2.29 us (5%)
    pallas_call x1, Pallas kernels, body(): pl.pallas_call(functools.partial(kernel, lefts, rights, group, cuts), out...  46.4 us
    unnamed x1, local copies, waits for them, and re-layouts  2.29 us

profile of v3, /device:TPU:0, one launch (start us, length us, event | category | flops | bytes accessed | tf_op | source)
XLA Modules:
  0.0 48.7 jit_solution(4928813127571044646)
XLA Ops:
  0.0 46.4 %shard_map.82 = f32[16,32,512]{2,1,0:T(8,128)} custom-call(f32[256,32,256]{2,1,0:T(8,128)} %signal.1, bf16[256,256]{1,0:T(8,128)(2,1)} %constant.8.clone.table_x, bf16[256,256]{1,0:T(8,128)(2,1)} %constant.9.clone.table_y, bf16[2,256,256]{2,1,0:T(8,128)(2,1)} %constant.10.clone.table_v, bf16[2,1024,512]{2,1,0:T(8,128)(2,1)} %constant.11.clone.table_w, ...), custom_call_target="tpu_custom_call" | custom-call | tf_op jit(solution)/shard_map/pallas_call | solution.py:323
  46.4 2.3 %copy.10 = f32[16,32,512]{2,1,0:T(8,128)} copy(f32[16,32,512]{2,1,0:T(8,128)} %shard_map.82) | data formatting | bytes 2097152

commit v4 on v3

--- a/solution.py
+++ b/solution.py
@@ -12,6 +12,7 @@
 LANES = 128
 ROWS = 8
 AHEAD = 2
+TILED = (1, 1)
 REST = 32
 
 
@@ -97,13 +98,18 @@
         for b in range(blocks):
             tile_copy(t, b).start()
 
-    def send_tile(t, o):
+    def send_tile(t, g, k, o):
         to = lax.bitwise_xor(left, o)
         return pltpu.make_async_remote_copy(
-            src_ref=first.at[t, 0, pl.ds(0, cuts[0]), to],
-            dst_ref=lines.at[left, t, pl.ds(0, cuts[0])],
-            send_sem=sent_left.at[0], recv_sem=came_left.at[0, 0],
+            src_ref=first.at[t, g, pl.ds(begins[k], cuts[k]), to],
+            dst_ref=lines.at[left, t, pl.ds(g * unit + begins[k], cuts[k])],
+            send_sem=sent_left.at[0], recv_sem=came_left.at[g, k],
             device_id=(to, right), device_id_type=MESH)
+
+    def send_tiles(t, g):
+        for k in pieces[: TILED[g]]:
+            for o in range(lefts - 1, 0, -1):
+                send_tile(t, g, k, o).start()
 
     def send_left(g, k, o):
         to = lax.bitwise_xor(left, o)
@@ -187,12 +193,11 @@
             copy_y.start()
             copy_w.start()
 
-        for o in range(lefts - 1, 0, -1):
-            send_tile(t, o).start()
+        send_tiles(t, 0)
         return carry
 
     lax.fori_loop(0, tiles, stage1, 0)
-    for k in pieces[1:]:
+    for k in pieces[TILED[0] :]:
         send_group(0, k)
     copy_y.wait()
 
@@ -208,7 +213,7 @@
         result = product(ty[...], split(values))
         for s in range(cuts[k]):
             second[at + s] = result[:, s * LANES : (s + 1) * LANES]
-        for o in range(rights - 1, 0, -1):
+        for o in sorted(range(1, rights), key=lambda o: (o == 1, o)):
             send_right(g, k, o).start()
         for s in range(cuts[k]):
             pencils[right, at + s] = second[at + s, pl.ds(pl.multiple_of(right * share_y, share_y), share_y), :]
@@ -217,6 +222,8 @@
 
     def later1(t, carry):
         transform(t, 1, groups, lambda y: (halves[t, y, 0], halves[t, y, 1]))
+        if groups > 1:
+            send_tiles(t, 1)
 
         @pl.when(t == min(1, tiles - 1))
         def _():
@@ -232,7 +239,10 @@
             send_group(g, k)
         return carry
 
-    lax.fori_loop(1, groups, start1, 0)
+    if groups > 1:
+        for k in pieces[TILED[1] :]:
+            send_group(1, k)
+    lax.fori_loop(2, groups, start1, 0)
     copy_w.wait()
 
     pick = lax.broadcasted_iota(jnp.int32, (share_y, symbol_y.shape[1]), 1) == (
@@ -305,7 +315,7 @@
     group = LANES // REST
     groups = share_x // group
     slots = share_x + groups
-    cuts = (2, 2, 1)
+    cuts = (2, 1, 1, 1)
     basis = half_band_basis(own_z, LANES + REST)
     rows_x = kept_table(size_x).T.reshape(lefts, groups, group, size_x).transpose(1, 2, 0, 3)
     rows_x = rows_x.reshape(groups, group * lefts, size_x)

time: 48.9 us -> 48.5 us (level)
  no operation moved by 1% of the time
where the time goes in v4:
time: 48.5 us; the launch traced here: 48.3 us
  Pallas kernels  46 us (95%)
  local copies, waits for them, and re-layouts  2.29 us (5%)
    pallas_call x1, Pallas kernels, body(): pl.pallas_call(functools.partial(kernel, lefts, rights, group, cuts), out...  46 us
    unnamed x1, local copies, waits for them, and re-layouts  2.29 us

profile of v4, /device:TPU:0, one launch (start us, length us, event | category | flops | bytes accessed | tf_op | source)
XLA Modules:
  0.0 48.3 jit_solution(2181868285276405936)
XLA Ops:
  0.0 46.0 %shard_map.82 = f32[16,32,512]{2,1,0:T(8,128)} custom-call(f32[256,32,256]{2,1,0:T(8,128)} %signal.1, bf16[256,256]{1,0:T(8,128)(2,1)} %constant.8.clone.table_x, bf16[256,256]{1,0:T(8,128)(2,1)} %constant.9.clone.table_y, bf16[2,256,256]{2,1,0:T(8,128)(2,1)} %constant.10.clone.table_v, bf16[2,1024,512]{2,1,0:T(8,128)(2,1)} %constant.11.clone.table_w, ...), custom_call_target="tpu_custom_call" | custom-call | tf_op jit(solution)/shard_map/pallas_call | solution.py:333
  46.0 2.3 %copy.10 = f32[16,32,512]{2,1,0:T(8,128)} copy(f32[16,32,512]{2,1,0:T(8,128)} %shard_map.82) | data formatting | bytes 2097152

commit v5 on v4

--- a/solution.py
+++ b/solution.py
@@ -61,7 +61,7 @@
 ):
     left, right = lax.axis_index("left"), lax.axis_index("right")
     tiles, blocks, size_x = held.shape[0], held.shape[1], held.shape[2]
-    groups, unit = first.shape[1], first.shape[2]
+    groups, unit = first.shape[1], first.shape[3]
     share_x = done.shape[0]
     size_y = lefts * tiles * ROWS
     modes_y = size_y // 2
@@ -101,7 +101,7 @@
     def send_tile(t, g, k, o):
         to = lax.bitwise_xor(left, o)
         return pltpu.make_async_remote_copy(
-            src_ref=first.at[t, g, pl.ds(begins[k], cuts[k]), to],
+            src_ref=first.at[t, g, to, pl.ds(begins[k], cuts[k])],
             dst_ref=lines.at[left, t, pl.ds(g * unit + begins[k], cuts[k])],
             send_sem=sent_left.at[0], recv_sem=came_left.at[g, k],
             device_id=(to, right), device_id_type=MESH)
@@ -114,7 +114,7 @@
     def send_left(g, k, o):
         to = lax.bitwise_xor(left, o)
         return pltpu.make_async_remote_copy(
-            src_ref=first.at[:, g, pl.ds(begins[k], cuts[k]), to],
+            src_ref=first.at[:, g, to, pl.ds(begins[k], cuts[k])],
             dst_ref=lines.at[left, :, pl.ds(g * unit + begins[k], cuts[k])],
             send_sem=sent_left.at[0], recv_sem=came_left.at[g, k],
             device_id=(to, right), device_id_type=MESH)
@@ -159,9 +159,9 @@
                 for j in range(group):
                     at = ((y * (high - low) + g - low) * group + j) * lefts
                     rows = result[at : at + lefts]
-                    view[pl.ds((1 + j) * lefts * ROWS + y, lefts, stride=ROWS), :] = rows[:, :LANES]
+                    view[pl.ds((1 + j) * ROWS + y, lefts, stride=unit * ROWS), :] = rows[:, :LANES]
                     packed = rows[:, LANES:] if j == 0 else jnp.where(lane_group == j, rows[:, LANES:], packed)
-                view[pl.ds(y, lefts, stride=ROWS), :] = packed
+                view[pl.ds(y, lefts, stride=unit * ROWS), :] = packed
 
     def send_group(g, k):
         for o in range(lefts - 1, 0, -1):
@@ -204,7 +204,7 @@
     def own(g):
         for t in range(tiles):
             for s in range(unit):
-                lines[left, t, g * unit + s] = first[t, g, s, left]
+                lines[left, t, g * unit + s] = first[t, g, left, s]
 
     def stage2(g, k):
         at = g * unit + begins[k]
@@ -342,7 +342,7 @@
             pltpu.VMEM(table_y.shape, jnp.bfloat16),
             pltpu.VMEM(table_v.shape, jnp.bfloat16),
             pltpu.VMEM(table_w.shape, jnp.bfloat16),
-            pltpu.VMEM((tiles, groups, group + 1, lefts, ROWS, LANES), jnp.float32),
+            pltpu.VMEM((tiles, groups, lefts, group + 1, ROWS, LANES), jnp.float32),
             pltpu.VMEM((lefts, tiles, slots, ROWS, LANES), jnp.float32),
             pltpu.VMEM((slots, modes_y, LANES), jnp.float32),
             pltpu.VMEM((rights, slots, share_y, LANES), jnp.float32),

time: 48.5 us -> 48.5 us (level)
  no operation moved by 1% of the time
where the time goes in v5:
time: 48.5 us; the launch traced here: 48.3 us
  Pallas kernels  46 us (95%)
  local copies, waits for them, and re-layouts  2.29 us (5%)
    pallas_call x1, Pallas kernels, body(): pl.pallas_call(functools.partial(kernel, lefts, rights, group, cuts), out...  46 us
    unnamed x1, local copies, waits for them, and re-layouts  2.29 us

profile of v5, /device:TPU:0, one launch (start us, length us, event | category | flops | bytes accessed | tf_op | source)
XLA Modules:
  0.0 48.3 jit_solution(5465170815563649026)
XLA Ops:
  0.0 46.0 %shard_map.82 = f32[16,32,512]{2,1,0:T(8,128)} custom-call(f32[256,32,256]{2,1,0:T(8,128)} %signal.1, bf16[256,256]{1,0:T(8,128)(2,1)} %constant.8.clone.table_x, bf16[256,256]{1,0:T(8,128)(2,1)} %constant.9.clone.table_y, bf16[2,256,256]{2,1,0:T(8,128)(2,1)} %constant.10.clone.table_v, bf16[2,1024,512]{2,1,0:T(8,128)(2,1)} %constant.11.clone.table_w, ...), custom_call_target="tpu_custom_call" | custom-call | tf_op jit(solution)/shard_map/pallas_call | solution.py:333
  46.0 2.3 %copy.10 = f32[16,32,512]{2,1,0:T(8,128)} copy(f32[16,32,512]{2,1,0:T(8,128)} %shard_map.82) | data formatting | bytes 2097152
